TPU v7x, 32 devices: a whole 2x2x4 slice. The times are simulated.
32 devices in a mesh: expert: 4 (over y, x), dp: 8 (over z, core).
Axes of the slice: x: 2, y: 2, z: 4, core: 2. Of those that a mesh axis runs over, the one named last changes fastest.
Arguments:
- acts: bfloat16 [32, 4, 16, 3584], P(('expert', 'dp')), may hold values from -6 to 6
- grad_out: bfloat16 [32, 4, 16, 1024], P(('expert', 'dp')), may hold values from -0.375 to 0.375
- routing_counts: int32 [32, 4], P(('expert', 'dp')), may hold values from 1 to 16, as said below
- left_basis: bfloat16 [4, 3584, 3584], P('expert', 'dp'), may hold values from -1 to 1, as said below
- right_basis: bfloat16 [4, 1024, 1024], P('expert'), may hold values from -1 to 1, as said below
- first_moment: float32 [4, 3584, 1024], P('expert', 'dp'), may hold values from -3 to 3
- second_moment: float32 [4, 3584, 1024], P('expert', 'dp'), may hold values from 0.05 to 2000
Outputs:
- step_delta: bfloat16 [4, 3584, 1024], P('expert', 'dp')
- first_out: float32 [4, 3584, 1024], P('expert', 'dp')
- second_out: float32 [4, 3584, 1024], P('expert', 'dp')
- expert_rms: float32 [4], P('expert')
Inputs may be any that keep to these rules, and one draw needn't show every extreme that they name: Slot s of shard i for expert e carries a routed token when s < routing_counts[i, e]; the other slots hold leftover values that belong to no token. In every shard some expert has all 16 slots live. `left_basis`: each expert's block is an orthogonal matrix rounded to bfloat16. `right_basis`: each expert's block is an orthogonal matrix rounded to bfloat16.
All inputs are finite; a program needn't handle non-finite values.
Results may differ from a plain program's by a relative error of at most 0.013.
Values may be sent and summed in bfloat16 or wider, within the bound.
A program may use at most 64 MiB of HBM per device.

v0:
```python
import jax
import jax.numpy as jnp
from jax import lax
from jax.sharding import PartitionSpec as P

BETA_ONE = 0.9
BETA_TWO = 0.95
EPS_DIVIDE = 1e-08
EPS_MEAN = 1e-06


def local(acts, grad_out, routing_counts, left_basis, right_basis, first_moment, second_moment):
    slot_count = acts.shape[2]
    slot_index = lax.broadcasted_iota(jnp.int32, routing_counts.shape + (slot_count,), 2)
    live_slots = (slot_index < routing_counts[:, :, None])[..., None]
    acts_live = jnp.where(live_slots, acts, jnp.zeros((), jnp.bfloat16))
    grads_live = jnp.where(live_slots, grad_out, jnp.zeros((), jnp.bfloat16))
    came_acts, came_grads = (
        lax.all_to_all(acts_live, "expert", split_axis=1, concat_axis=0, tiled=True),
        lax.all_to_all(grads_live, "expert", split_axis=1, concat_axis=0, tiled=True),
    )
    model_width = came_acts.shape[-1]
    hidden_width = came_grads.shape[-1]
    column_slabs = lax.all_to_all(came_acts, "dp", split_axis=3, concat_axis=0, tiled=True)
    grad_slabs = lax.all_gather(came_grads, "dp", axis=0, tiled=True)
    source_count = lax.axis_size("dp")
    column_slabs = column_slabs.reshape(source_count, -1, column_slabs.shape[-1])
    grad_slabs = grad_slabs.reshape(source_count, -1, hidden_width)
    partials = jnp.einsum(
        "stk,stf->skf", column_slabs, grad_slabs, preferred_element_type=jnp.float32
    )
    partials = lax.optimization_barrier(partials.astype(jnp.bfloat16))
    summed = jnp.sum(partials.astype(jnp.float32), axis=0)
    gradient = summed.astype(jnp.bfloat16)
    right_block = right_basis[0]
    left_rows = left_basis[0]
    right_turned = jnp.dot(gradient, right_block, preferred_element_type=jnp.float32).astype(
        jnp.bfloat16
    )
    basis_columns = left_rows
    rotated = lax.psum_scatter(
        jnp.einsum(
            "kc,kf->cf", basis_columns, right_turned, preferred_element_type=jnp.float32
        ).astype(jnp.bfloat16),
        "dp",
        scatter_dimension=0,
        tiled=True,
    ).astype(jnp.float32)
    first_new = BETA_ONE * first_moment[0] + (1.0 - BETA_ONE) * rotated
    second_new = BETA_TWO * second_moment[0] + (1.0 - BETA_TWO) * rotated * rotated
    direction = (first_new / (jnp.sqrt(second_new) + EPS_DIVIDE)).astype(jnp.bfloat16)
    restored = jnp.einsum(
        "kg,fg->kf", direction, right_block, preferred_element_type=jnp.float32
    ).astype(jnp.bfloat16)
    basis_columns = left_rows
    update = jnp.dot(
        basis_columns,
        lax.all_gather(restored, "dp", axis=0, tiled=True),
        preferred_element_type=jnp.float32,
    )
    squares = jnp.sum(update * update)
    cell_total = float(model_width * hidden_width)
    total_squares = lax.psum(squares, "dp")
    own_norm = jnp.sqrt(total_squares / cell_total + EPS_MEAN)
    norm_total = lax.psum(own_norm, "expert")
    mean_norm = norm_total / lax.axis_size("expert")
    step_delta = (-update / jnp.maximum(own_norm, mean_norm)).astype(jnp.bfloat16)
    return (step_delta[None], first_new[None], second_new[None], own_norm.reshape(1))


def solution(mesh):
    in_specs = (
        P(("expert", "dp"), None, None, None),
        P(("expert", "dp"), None, None, None),
        P(("expert", "dp"), None),
        P("expert", "dp", None),
        P("expert", None, None),
        P("expert", "dp", None),
        P("expert", "dp", None),
    )
    out_specs = (
        P("expert", "dp", None),
        P("expert", "dp", None),
        P("expert", "dp", None),
        P("expert"),
    )
    return jax.shard_map(local, mesh=mesh, in_specs=in_specs, out_specs=out_specs, check_vma=False)
```

profile of v0, /device:TPU:0, one launch (start us, length us, event | category | flops | bytes accessed | tf_op | source)
XLA Modules:
  0.0 312.0 jit_solution(15991708466216752481)
XLA Ops:
  7.2 0.0 all-gather.6.cloned.1.call-start
  7.2 0.9 iota_compare_fusion
  8.1 1.0 bitcast_select_fusion.1
  9.1 10.1 %all_to_all.39 = bf16[1,4,16,1024]{3,2,0,1:T(8,128)(2,1)} all-to-all(bf16[1,4,16,1024]{3,2,0,1:T(8,128)(2,1)S(1)} %bitcast_select_fusion.1), channel_id=1, replica_groups=mesh['expert'=4,'dp'=8] {'expert'}, dimensions={1} | all-to-all | bytes 262144 | tf_op jit(solution)/shard_map/all_to_all | solution.py:20
  19.3 0.0 all-gather.6.cloned.1.call-update
  19.3 0.0 reduce-scatter.4.cloned.1.call-start
  19.3 1.1 bitcast_select_fusion
  20.5 10.0 %all_to_all.40 = bf16[1,4,16,3584]{3,2,0,1:T(8,128)(2,1)} all-to-all(bf16[1,4,16,3584]{3,2,0,1:T(8,128)(2,1)S(1)} %bitcast_select_fusion), channel_id=1, replica_groups=mesh['expert'=4,'dp'=8] {'expert'}, dimensions={1} | all-to-all | bytes 917504 | tf_op jit(solution)/shard_map/all_to_all | solution.py:19
  30.5 5.3 %copy.31 = bf16[4,1,16,3584]{2,0,1,3:T(4,128)(2,1)} copy(bf16[4,1,16,3584]{3,2,0,1:T(8,128)(2,1)} %bitcast.64) | data formatting | bytes 917504 | tf_op jit(solution)/shard_map/all_to_all | solution.py:19
  35.8 6.0 %reshape.63 = bf16[8,2,14336]{2,1,0:T(2,128)(2,1)} reshape(bf16[3584,1,4,16]{3,2,1,0:T(4,128)(2,1)} %bitcast.60) | data formatting | bytes 917504
  41.7 18.9 %all_to_all.41 = bf16[8,2,14336]{2,1,0:T(2,128)(2,1)} all-to-all(bf16[8,2,14336]{2,1,0:T(2,128)(2,1)} %reshape.63), channel_id=1, replica_groups=mesh['expert'=4,'dp'=8] {'dp'}, dimensions={0} | all-to-all | bytes 917504 | tf_op jit(solution)/shard_map/all_to_all | solution.py:24
  60.7 5.1 %reshape.64 = bf16[3584,1,4,16]{3,2,1,0:T(4,128)(2,1)} reshape(bf16[8,2,14336]{2,1,0:T(2,128)(2,1)} %all_to_all.41) | data formatting | bytes 917504
  65.7 5.1 %copy.38 = bf16[4,1,16,8,448]{4,3,2,0,1:T(8,128)(2,1)} copy(bf16[4,1,16,8,448]{2,0,4,3,1:T(4,128)(2,1)} %bitcast.61) | data formatting | bytes 917504 | tf_op jit(solution)/shard_map/all_to_all | solution.py:24
  70.8 2.0 copy.33
  72.8 6.5 %convolution_convert_fusion.1 = bf16[8,448,1024]{2,1,0:T(8,128)(2,1)} fusion(bf16[8,64,448]{2,1,0:T(8,128)(2,1)} %bitcast.62, bf16[8,64,1024]{2,1,0:T(8,128)(2,1)} %bitcast.65), kind=kOutput, calls=%fused_computation.2 | convolution fusion | flops 473432064 | bytes 8847360 | tf_op jit(solution)/shard_map/stk,stf->skf/dot_general | solution.py:29
  79.3 6.0 %reduce_sum.21 = bf16[448,1024]{1,0:T(8,128)(2,1)} reduce(bf16[8,448,1024]{2,1,0:T(8,128)(2,1)} %convolution_convert_fusion.1, bf16[]{:T(256)} %constant.4.clone.1), dimensions={0}, to_apply=%region_0.1 | reduce | flops 3211264 | bytes 8257538 | tf_op jit(solution)/shard_map/reduce_sum | solution.py:33
  85.3 9.9 %fusion = bf16[3584,1024]{0,1:T(8,128)(2,1)} fusion(bf16[1,448,3584]{2,1,0:T(8,128)(2,1)S(1)} %copy-done, bf16[448,1024]{1,0:T(8,128)(2,1)} %reduce_sum.21, bf16[1,1024,1024]{2,1,0:T(8,128)(2,1)} %param.11), kind=kOutput, calls=%fused_computation.1 | convolution fusion | flops 4231987200 | bytes 13565952 | tf_op jit(solution)/shard_map/kc,kf->cf/dot_general | solution.py:42
  95.2 10.4 %copy.39 = bf16[3584,1024]{1,0:T(8,128)(2,1)} copy(bf16[3584,1024]{0,1:T(8,128)(2,1)} %fusion) | data formatting | bytes 14680064
  105.6 0.2 all-gather.4.cloned.1.call-start
  105.9 2.9 copy.29
  108.8 3.0 copy.35
  111.8 70.9 %reduce-scatter.4.cloned.1.call-done = bf16[448,1024]{1,0:T(8,128)(2,1)} async-done(((bf16[3584,1024]{1,0:T(8,128)(2,1)}), bf16[448,1024]{1,0:T(8,128)(2,1)}) %reduce-scatter.4.cloned.1.call-update) | async-done | bytes 917520
  182.6 2.2 copy.40
  184.9 6.4 %fusion.13 = bf16[448,1024]{1,0:T(8,128)(2,1)} fusion(bf16[1,1024,1024]{2,1,0:T(8,128)(2,1)} %param.11, bf16[448,1024]{0,1:T(8,128)(2,1)} %copy.40, f32[1,448,1024]{1,2,0:T(8,128)} %copy.29, f32[1,448,1024]{1,2,0:T(8,128)} %copy.35), kind=kOutput, calls=%fused_computation.18 | convolution fusion | flops 945029120 | bytes 7602176 | tf_op jit(solution)/shard_map/kg,fg->kf/dot_general | solution.py:52
  191.3 5.4 %fusion.17 = (f32[1,448,1024]{1,2,0:T(8,128)}, f32[1,448,1024]{1,2,0:T(8,128)}) fusion(bf16[448,1024]{0,1:T(8,128)(2,1)} %copy.40, f32[1,448,1024]{1,2,0:T(8,128)} %copy.35, f32[1,448,1024]{1,2,0:T(8,128)} %copy.29), kind=kLoop, calls=%fused_computation.20 | loop fusion | flops 3670016 | bytes 8257536 | tf_op jit(solution)/shard_map/broadcast_in_dim | solution.py:68
  196.7 3.0 copy.36
  199.7 63.6 %all-gather.4.cloned.1.call-done = bf16[3584,1024]{1,0:T(8,128)(2,1)} async-done(((bf16[448,1024]{1,0:T(8,128)(2,1)}), bf16[3584,1024]{1,0:T(8,128)(2,1)}) %all-gather.4.cloned.1.call-update) | async-done | bytes 7340048 | tf_op jit(solution)/shard_map/all_gather | solution.py:58
  263.3 8.4 %multiply_reduce_fusion = (f32[]{:T(128)}, f32[1024,448]{0,1:T(8,128)}) fusion(bf16[3584,1024]{1,0:T(8,128)(2,1)} %all-gather.4.cloned.1.call-done, bf16[1,448,3584]{2,1,0:T(8,128)(2,1)S(1)} %copy-done), kind=kOutput, calls=%fused_computation.16 | convolution fusion | flops 3289251840 | bytes 12386308 | tf_op jit(solution)/shard_map/dot_general | solution.py:56
  271.6 14.7 %psum.14 = f32[]{:T(128)} all-reduce(f32[]{:T(128)} %get-tuple-element.22), channel_id=1, replica_groups=mesh['expert'=4,'dp'=8] {'dp'}, use_global_device_ids=true, to_apply=%region_3.4 | all-reduce | flops 1 | bytes 8 | tf_op jit(solution)/shard_map/psum | solution.py:63
  287.0 2.8 copy.37
  289.8 11.2 %psum.15 = f32[]{:T(128)} all-reduce(f32[]{:T(128)} %sqrt.7), channel_id=1, replica_groups=mesh['expert'=4,'dp'=8] {'expert'}, use_global_device_ids=true, to_apply=%region_4.5 | all-reduce | flops 1 | bytes 8 | tf_op jit(solution)/shard_map/psum | solution.py:65
  301.7 2.6 fusion.18
  (5 shorter events, 0.0 us)
Async XLA Ops:
  7.2 78.1 %copy-start = (bf16[1,448,3584]{2,1,0:T(8,128)(2,1)S(1)}, bf16[1,448,3584]{2,1,0:T(8,128)(2,1)}, u32[]{:S(2)}) copy-start(bf16[1,448,3584]{2,1,0:T(8,128)(2,1)} %param.10) | copy-start | bytes 9633796
  7.2 65.7 %all-gather.6.cloned.1.call-start = ((), (), s32[]{:S(2)}) async-start(), calls=%async_computation.5 | async-start | bytes 1179648 | tf_op jit(solution)/shard_map/all_gather | solution.py:25
  19.3 163.3 %reduce-scatter.4.cloned.1.call-start = ((), (), s32[]{:S(2)}) async-start(), calls=%async_computation.6 | async-start | bytes 8257536
  105.6 157.7 %all-gather.4.cloned.1.call-start = ((), (), s32[]{:S(2)}) async-start(), calls=%async_computation.4 | async-start | bytes 8257536 | tf_op jit(solution)/shard_map/all_gather | solution.py:58
Sparse Core Ops, SparseCore 0:
  19.4 21.7 all-gather.5
  105.7 76.8 reduce-scatter.3
  191.4 71.7 all-gather.3
where the time goes:
time: 313 us; the launch traced here: 312 us
  waiting for transfers between devices  134 us (43%)
  blocking collectives  65 us (21%)
  local copies, waits for them, and re-layouts  47.8 us (15%)
  matrix products  31.1 us (10%)
  other arithmetic  17.1 us (5%)
  between operations  16.3 us (5%)
    unnamed x4, waiting for transfers between devices  70.9 us
    all_gather x1, waiting for transfers between devices, local(): lax.all_gather(restored, 'dp', axis=0, tiled=True)  63.6 us
    unnamed x10, local copies, waits for them, and re-layouts  35.4 us
    all_to_all x1, blocking collectives, local(): lax.all_to_all(came_acts, 'dp', split_axis=3, concat_axis=0, tiled=True)  18.9 us
    psum x1, blocking collectives, local(): total_squares = lax.psum(squares, 'dp')  14.7 us
    psum x1, blocking collectives, local(): norm_total = lax.psum(own_norm, 'expert')  11.2 us
    all_to_all x1, blocking collectives, local(): lax.all_to_all(grads_live, 'expert', split_axis=1, concat_axis=0, tiled=T...  10.1 us
    all_to_all x1, blocking collectives, local(): lax.all_to_all(acts_live, 'expert', split_axis=1, concat_axis=0, tiled=True)  10 us
  transfers between devices with their start and end apart: 3, of which 2 were waited for; matrix products, arithmetic and copies ran while one was open for 12% of the time, Pallas kernels for 0%

commit v1 on v0

--- a/solution.py
+++ b/solution.py
@@ -21,7 +21,10 @@
     )
     model_width = came_acts.shape[-1]
     hidden_width = came_grads.shape[-1]
-    column_slabs = lax.all_to_all(came_acts, "dp", split_axis=3, concat_axis=0, tiled=True)
+    column_slabs = jnp.concatenate(
+        lax.all_to_all(jnp.stack(jnp.split(came_acts, lax.axis_size("dp"), axis=3)), "dp", 0, 0),
+        axis=0,
+    )
     grad_slabs = lax.all_gather(came_grads, "dp", axis=0, tiled=True)
     source_count = lax.axis_size("dp")
     column_slabs = column_slabs.reshape(source_count, -1, column_slabs.shape[-1])

time: 313 us -> 303 us (0.968)
  blocking collectives: 65 us -> 48.6 us
  local copies, waits for them, and re-layouts: 47.8 us -> 31.5 us
  waiting for transfers between devices: 134 us -> 146 us
  starting transfers between devices: 0.3 us -> 9.61 us
    all_to_all x3 -> x1, blocking collectives: 39.1 us -> 22.7 us  [local(): lax.all_to_all(jnp.stack(jnp.split(came_acts, lax.axis_size('dp'), axis=3...]
    all_to_all x3 -> x0, local copies, waits for them, and re-layouts: 12.4 us -> none  [the longest x2 7.1 us: local(): lax.all_to_all(came_acts, 'dp', split_axis=3, concat_axis=0, tiled=True)]
    all_to_all x0 -> x2, starting transfers between devices: none -> 9.31 us  [the longest x1 5.19 us: local(): lax.all_to_all(grads_live, 'expert', split_axis=1, concat_axis=0, tiled=T...]
    all_to_all x0 -> x2, waiting for transfers between devices: none -> 8.64 us  [the longest x1 5.5 us: local(): lax.all_to_all(acts_live, 'expert', split_axis=1, concat_axis=0, tiled=True)]
    unnamed x10 -> x17, local copies, waits for them, and re-layouts: 35.4 us -> 30.5 us
  transfers between devices with their start and end apart: 3 -> 5, of which waited for: 2 -> 4; matrix products, arithmetic and copies ran while one was open for 12% -> 8% of each run, Pallas kernels for 0% -> 0%
where the time goes in v1:
time: 303 us; the launch traced here: 302 us
  waiting for transfers between devices  146 us (48%)
  blocking collectives  48.6 us (16%)
  local copies, waits for them, and re-layouts  31.5 us (10%)
  matrix products  31.1 us (10%)
  other arithmetic  18.5 us (6%)
  between operations  16.3 us (5%)
  starting transfers between devices  9.61 us (3%)
    unnamed x4, waiting for transfers between devices  73.7 us
    all_gather x1, waiting for transfers between devices, local(): lax.all_gather(restored, 'dp', axis=0, tiled=True)  63.6 us
    unnamed x17, local copies, waits for them, and re-layouts  30.5 us
    all_to_all x1, blocking collectives, local(): lax.all_to_all(jnp.stack(jnp.split(came_acts, lax.axis_size('dp'), axis=3...  22.7 us
    psum x1, blocking collectives, local(): total_squares = lax.psum(squares, 'dp')  14.7 us
    psum x1, blocking collectives, local(): norm_total = lax.psum(own_norm, 'expert')  11.2 us
    dot_general x1, matrix products, local(): jnp.einsum('kc,kf->cf', basis_columns, right_turned, preferred_element_ty...  9.91 us
    dot_general x1, matrix products, local(): jnp.dot(basis_columns, lax.all_gather(restored, 'dp', axis=0, tiled=True)...  8.39 us
  transfers between devices with their start and end apart: 5, of which 4 were waited for; matrix products, arithmetic and copies ran while one was open for 8% of the time, Pallas kernels for 0%

profile of v1, /device:TPU:0, one launch (start us, length us, event | category | flops | bytes accessed | tf_op | source)
XLA Modules:
  0.0 301.6 jit_solution(18418282786657525008)
XLA Ops:
  7.2 0.9 iota_compare_fusion
  8.1 1.7 bitcast_select_fusion.1
  9.8 5.2 %all-to-all-start.2 = ((bf16[1,4,16,1024]{3,2,0,1:T(8,128)(2,1)}), bf16[1,4,16,1024]{3,2,0,1:T(8,128)(2,1)S(1)}, u32[]{:S(2)}, u32[]{:S(2)}) async-start(bf16[1,4,16,1024]{3,2,0,1:T(8,128)(2,1)} %bitcast_select_fusion.1), calls=%async_computation.2 | async-start | bytes 262144 | tf_op jit(solution)/shard_map/all_to_all | solution.py:20
  15.0 1.9 bitcast_select_fusion
  16.9 3.1 %all-to-all-done.2 = bf16[1,4,16,1024]{3,2,0,1:T(8,128)(2,1)S(1)} async-done(((bf16[1,4,16,1024]{3,2,0,1:T(8,128)(2,1)}), bf16[1,4,16,1024]{3,2,0,1:T(8,128)(2,1)S(1)}, u32[]{:S(2)}, u32[]{:S(2)}) %all-to-all-start.2) | async-done | bytes 131104 | tf_op jit(solution)/shard_map/all_to_all | solution.py:20
  20.0 4.1 %all-to-all-start = ((bf16[1,4,16,3584]{3,2,0,1:T(8,128)(2,1)}), bf16[1,4,16,3584]{3,2,0,1:T(8,128)(2,1)}, u32[]{:S(2)}, u32[]{:S(2)}) async-start(bf16[1,4,16,3584]{3,2,0,1:T(8,128)(2,1)} %bitcast_select_fusion), calls=%async_computation | async-start | bytes 917504 | tf_op jit(solution)/shard_map/all_to_all | solution.py:19
  24.9 5.5 %all-to-all-done = bf16[1,4,16,3584]{3,2,0,1:T(8,128)(2,1)} async-done(((bf16[1,4,16,3584]{3,2,0,1:T(8,128)(2,1)}), bf16[1,4,16,3584]{3,2,0,1:T(8,128)(2,1)}, u32[]{:S(2)}, u32[]{:S(2)}) %all-to-all-start) | async-done | bytes 458784 | tf_op jit(solution)/shard_map/all_to_all | solution.py:19
  31.3 1.0 fusion.27
  32.2 0.8 fusion.26
  33.1 1.0 fusion.25
  34.1 0.8 fusion.24
  34.9 1.0 fusion.23
  35.9 0.8 fusion.22
  36.7 0.9 fusion.21
  37.7 22.7 %all_to_all.29 = bf16[8,4,1,16,448]{4,3,1,2,0:T(8,128)(2,1)} all-to-all(bf16[8,4,1,16,448]{4,3,1,2,0:T(8,128)(2,1)S(1)} %fusion.21), channel_id=1, replica_groups=mesh['expert'=4,'dp'=8] {'dp'}, dimensions={0} | all-to-all | bytes 917504 | tf_op jit(solution)/shard_map/all_to_all | solution.py:25
  60.4 6.4 %convolution_convert_fusion.1 = bf16[8,448,1024]{2,1,0:T(8,128)(2,1)} fusion(bf16[8,64,448]{2,1,0:T(8,128)(2,1)} %bitcast.88, bf16[8,64,1024]{2,1,0:T(8,128)(2,1)} %bitcast.89), kind=kOutput, calls=%fused_computation.2 | convolution fusion | flops 473432064 | bytes 8847360 | tf_op jit(solution)/shard_map/stk,stf->skf/dot_general | solution.py:32
  66.9 6.0 %reduce_sum.21 = bf16[448,1024]{1,0:T(8,128)(2,1)} reduce(bf16[8,448,1024]{2,1,0:T(8,128)(2,1)} %convolution_convert_fusion.1, bf16[]{:T(256)} %constant.4.clone.1), dimensions={0}, to_apply=%region_0.1 | reduce | flops 3211264 | bytes 8257538 | tf_op jit(solution)/shard_map/reduce_sum | solution.py:36
  72.9 9.9 %fusion = bf16[3584,1024]{0,1:T(8,128)(2,1)} fusion(bf16[1,448,3584]{2,1,0:T(8,128)(2,1)S(1)} %copy-done, bf16[448,1024]{1,0:T(8,128)(2,1)} %reduce_sum.21, bf16[1,1024,1024]{2,1,0:T(8,128)(2,1)} %param.11), kind=kOutput, calls=%fused_computation.1 | convolution fusion | flops 4231987200 | bytes 13565952 | tf_op jit(solution)/shard_map/kc,kf->cf/dot_general | solution.py:45
  82.8 10.4 %copy.21 = bf16[3584,1024]{1,0:T(8,128)(2,1)} copy(bf16[3584,1024]{0,1:T(8,128)(2,1)} %fusion) | data formatting | bytes 14680064
  93.4 2.9 copy.15
  96.4 2.8 copy.18
  99.2 73.0 %reduce-scatter.4.cloned.1.call-done = bf16[448,1024]{1,0:T(8,128)(2,1)} async-done(((bf16[3584,1024]{1,0:T(8,128)(2,1)}), bf16[448,1024]{1,0:T(8,128)(2,1)}) %reduce-scatter.4.cloned.1.call-update) | async-done | bytes 917520
  172.2 2.2 copy.22
  174.4 6.4 %fusion.13 = bf16[448,1024]{1,0:T(8,128)(2,1)} fusion(bf16[1,1024,1024]{2,1,0:T(8,128)(2,1)} %param.11, bf16[448,1024]{0,1:T(8,128)(2,1)} %copy.22, f32[1,448,1024]{1,2,0:T(8,128)} %copy.15, f32[1,448,1024]{1,2,0:T(8,128)} %copy.18), kind=kOutput, calls=%fused_computation.18 | convolution fusion | flops 945029120 | bytes 7602176 | tf_op jit(solution)/shard_map/kg,fg->kf/dot_general | solution.py:55
  180.9 5.4 %fusion.17 = (f32[1,448,1024]{1,2,0:T(8,128)}, f32[1,448,1024]{1,2,0:T(8,128)}) fusion(bf16[448,1024]{0,1:T(8,128)(2,1)} %copy.22, f32[1,448,1024]{1,2,0:T(8,128)} %copy.18, f32[1,448,1024]{1,2,0:T(8,128)} %copy.15), kind=kLoop, calls=%fused_computation.20 | loop fusion | flops 3670016 | bytes 8257536 | tf_op jit(solution)/shard_map/broadcast_in_dim | solution.py:71
  186.3 3.0 copy.19
  189.3 63.6 %all-gather.4.cloned.1.call-done = bf16[3584,1024]{1,0:T(8,128)(2,1)} async-done(((bf16[448,1024]{1,0:T(8,128)(2,1)}), bf16[3584,1024]{1,0:T(8,128)(2,1)}) %all-gather.4.cloned.1.call-update) | async-done | bytes 7340048 | tf_op jit(solution)/shard_map/all_gather | solution.py:61
  252.8 8.4 %multiply_reduce_fusion = (f32[]{:T(128)}, f32[1024,448]{0,1:T(8,128)}) fusion(bf16[3584,1024]{1,0:T(8,128)(2,1)} %all-gather.4.cloned.1.call-done, bf16[1,448,3584]{2,1,0:T(8,128)(2,1)S(1)} %copy-done), kind=kOutput, calls=%fused_computation.16 | convolution fusion | flops 3289251840 | bytes 12386308 | tf_op jit(solution)/shard_map/dot_general | solution.py:59
  261.2 14.7 %psum.14 = f32[]{:T(128)} all-reduce(f32[]{:T(128)} %get-tuple-element.14), channel_id=1, replica_groups=mesh['expert'=4,'dp'=8] {'dp'}, use_global_device_ids=true, to_apply=%region_3.4 | all-reduce | flops 1 | bytes 8 | tf_op jit(solution)/shard_map/psum | solution.py:66
  276.6 2.8 copy.20
  279.4 11.2 %psum.15 = f32[]{:T(128)} all-reduce(f32[]{:T(128)} %sqrt.7), channel_id=1, replica_groups=mesh['expert'=4,'dp'=8] {'expert'}, use_global_device_ids=true, to_apply=%region_4.5 | all-reduce | flops 1 | bytes 8 | tf_op jit(solution)/shard_map/psum | solution.py:68
  291.3 2.6 fusion.18
  (12 shorter events, 1.9 us)
Async XLA Ops:
  7.2 65.7 %copy-start = (bf16[1,448,3584]{2,1,0:T(8,128)(2,1)S(1)}, bf16[1,448,3584]{2,1,0:T(8,128)(2,1)}, u32[]{:S(2)}) copy-start(bf16[1,448,3584]{2,1,0:T(8,128)(2,1)} %param.10) | copy-start | bytes 9633796
  9.8 10.2 %all-to-all-start.2 = ((bf16[1,4,16,1024]{3,2,0,1:T(8,128)(2,1)}), bf16[1,4,16,1024]{3,2,0,1:T(8,128)(2,1)S(1)}, u32[]{:S(2)}, u32[]{:S(2)}) async-start(bf16[1,4,16,1024]{3,2,0,1:T(8,128)(2,1)} %bitcast_select_fusion.1), calls=%async_computation.2 | async-start | bytes 262144 | tf_op jit(solution)/shard_map/all_to_all | solution.py:20
  20.0 4.2 %copy-start.1 = (bf16[1,4,16,1024]{3,2,0,1:T(8,128)(2,1)}, bf16[1,4,16,1024]{3,2,0,1:T(8,128)(2,1)S(1)}, u32[]{:S(2)}) copy-start(bf16[1,4,16,1024]{3,2,0,1:T(8,128)(2,1)S(1)} %all-to-all-done.2) | copy-start | bytes 393220
  20.0 10.4 %all-to-all-start = ((bf16[1,4,16,3584]{3,2,0,1:T(8,128)(2,1)}), bf16[1,4,16,3584]{3,2,0,1:T(8,128)(2,1)}, u32[]{:S(2)}, u32[]{:S(2)}) async-start(bf16[1,4,16,3584]{3,2,0,1:T(8,128)(2,1)} %bitcast_select_fusion), calls=%async_computation | async-start | bytes 917504 | tf_op jit(solution)/shard_map/all_to_all | solution.py:19
  24.1 36.3 %all-gather.6.cloned.1.call-start = ((), (), s32[]{:S(2)}) async-start(), calls=%async_computation.5 | async-start | bytes 1179648 | tf_op jit(solution)/shard_map/all_gather | solution.py:28
  24.9 147.3 %reduce-scatter.4.cloned.1.call-start = ((), (), s32[]{:S(2)}) async-start(), calls=%async_computation.6 | async-start | bytes 8257536
  93.2 159.7 %all-gather.4.cloned.1.call-start = ((), (), s32[]{:S(2)}) async-start(), calls=%async_computation.4 | async-start | bytes 8257536 | tf_op jit(solution)/shard_map/all_gather | solution.py:61
Sparse Core Ops, SparseCore 0:
  27.1 28.3 all-gather.5
  93.3 78.8 reduce-scatter.3
  181.0 71.8 all-gather.3
